TPU v7x, 128 devices: a whole 4x4x4 slice. The times are simulated.
128 devices in a mesh: img: 32 (over y, z, core), grp: 4 (over x).
Axes of the slice: x: 4, y: 4, z: 4, core: 2. Of those that a mesh axis runs over, the one named last changes fastest.
Arguments:
- images: bfloat16 [49152, 9216], P(('img', 'grp')), may hold values from -64 to 64, as said below
- expansion_basis: bfloat16 [9216, 960], P(None, 'img'), may hold values from -0.0625 to 0.0625
- block_sizes: int32 [16], replicated, may hold values from 1 to 80, 480 in all
- keep_count: int32 [16], replicated, may hold values from 1 to 8
- start_block: float32 [16, 80, 8], replicated, may hold values from -6 to 6
Outputs:
- features: float32 [49152, 256], P(('img', 'grp'))
- values: float32 [16, 8], replicated
Inputs may be any that keep to these rules, and one draw needn't show every extreme that they name: `images`: pixel values of order one. `block_sizes`: the 16 sizes sum to 480.
All inputs are finite; a program needn't handle non-finite values.
Results may differ from a plain program's by a relative error of at most 0.025.
Values may be sent and summed in bfloat16 or wider, within the bound.
A program may use at most 128 MiB of HBM per device.

v0:
```python
import jax
import jax.numpy as jnp
from jax import lax
from jax.sharding import Mesh
from jax.sharding import PartitionSpec as P

NMAX = 80
L = 16
S = 480
KMAX = 8
ITERS = 3
IMG = ("img_0", "img_1", "img_2")
IMG_GRP = ("img_0", "img_1", "img_2", "grp")
HIGH = lax.Precision.HIGHEST


def cut_along(shard, dim, peers):
    shape = shard.shape
    tiles = shard.reshape(*shape[:dim], peers, shape[dim] // peers, *shape[dim + 1 :])
    return jnp.moveaxis(tiles, dim, 0)


def sum_at_owner(shard, axis, dim):
    peers = lax.axis_size(axis)
    tiles = lax.all_to_all(cut_along(shard, dim, peers), axis, 0, 0, tiled=True)
    return jnp.sum(tiles, axis=0)


def summed_rows(shard, axes, dim):
    far, near = axes
    tiles = cut_along(shard, dim, lax.axis_size(far))
    nearer = sum_at_owner(tiles, near, dim + 1)
    arrived = lax.all_to_all(nearer, far, split_axis=0, concat_axis=0, tiled=True)
    return arrived.sum(axis=0)


def padded_to(lines, peers):
    spare = -len(lines) % peers
    return jnp.pad(lines, [(0, spare)] + [(0, 0)] * (lines.ndim - 1))


def sent_to_all(shard, axis):
    peers = lax.axis_size(axis)
    return lax.all_to_all(
        jnp.broadcast_to(shard[None], (peers, *shard.shape)), axis, 0, 0, tiled=True
    )


def in_order(tiles, dim):
    shape = list(tiles.shape[1:])
    shape[dim] *= tiles.shape[0]
    return jnp.moveaxis(tiles, 0, dim).reshape(shape)


def gather_axes(shard, axes, dim):
    far, near = axes
    leading = sent_to_all(shard, far)
    tiles = jnp.swapaxes(sent_to_all(leading, near), 0, 1)
    return in_order(tiles.reshape(-1, *shard.shape), dim)


def nested_sum(shard, axes):
    lines = shard.reshape(-1, shard.shape[-1])
    own = summed_rows(padded_to(lines, lax.axis_size(axes[0]) * lax.axis_size(axes[1])), axes, 0)
    whole = gather_axes(own, axes, 0)
    return whole[: len(lines)].reshape(shard.shape)


def selector(block_sizes, total, count, width):
    offsets = jnp.cumsum(block_sizes) - block_sizes
    column = jnp.arange(total, dtype=jnp.int32)[:, None, None]
    inside = jnp.arange(width, dtype=jnp.int32)[None, None, :]
    hit = (column == offsets[None, :, None] + inside) & (inside < block_sizes[None, :, None])
    return hit.astype(jnp.bfloat16).reshape(total, count * width)


def subspace(cover, block_sizes, keep_count, start_block):
    width = cover.shape[1]
    ranks = start_block.shape[2]
    inside = jnp.arange(width, dtype=jnp.int32)[None, :, None] < block_sizes[:, None, None]
    keep = jnp.minimum(keep_count, (block_sizes + 1) // 2)
    current = jnp.where(inside, start_block, jnp.zeros_like(start_block))
    for turn in range(ITERS):
        product = jnp.einsum("bij,bjk->bik", cover, current, precision=HIGH)
        columns = []
        for column_id in range(ranks):
            vector = product[:, :, column_id]
            for earlier in columns:
                vector = vector - jnp.sum(earlier * vector, axis=1, keepdims=True) * earlier
            length = jnp.sqrt(jnp.sum(vector * vector, axis=1, keepdims=True))
            alive = (column_id < keep)[:, None]
            columns.append(jnp.where(alive, vector / length, jnp.zeros_like(vector)))
        current = jnp.stack(columns, axis=2)
    product = jnp.einsum("bij,bjk->bik", cover, current, precision=HIGH)
    found = jnp.sum(current * product, axis=1)
    return (current, found)


def per_device(images, expansion_basis, block_sizes, keep_count, start_block):
    rows = images.shape[0]
    coeffs = jnp.dot(
        images,
        lax.all_gather(expansion_basis, IMG, axis=1, tiled=True),
        preferred_element_type=jnp.float32,
    ).astype(jnp.bfloat16)
    samples = coeffs.reshape(2 * rows, S)
    pick = selector(block_sizes, S, L, NMAX)
    padded = jnp.dot(samples, pick, preferred_element_type=jnp.float32).astype(jnp.bfloat16)
    wide = padded.reshape(2 * rows, L, NMAX)
    scale = 1.0 / (2 * rows * lax.axis_size(IMG) * lax.axis_size("grp"))
    partial_value = (
        jnp.einsum("rli,rlj->lij", wide, wide, preferred_element_type=jnp.float32) * scale
    )
    cover = nested_sum(partial_value, (("img_0", "img_1"), ("img_2", "grp")))
    vectors, found = subspace(cover, block_sizes, keep_count, start_block)
    rounded = vectors.astype(jnp.bfloat16)
    features = jnp.einsum("rli,lij->rlj", wide, rounded, preferred_element_type=jnp.float32)
    return (features.reshape(rows, 2 * L * KMAX), found)


def solution(mesh):
    split = Mesh(
        mesh.devices.reshape(4, 4, 2, mesh.shape["grp"]), ("img_0", "img_1", "img_2", "grp")
    )
    in_specs = (P(IMG_GRP, None), P(None, IMG), P(), P(), P())
    out_specs = (P(IMG_GRP, None), P())
    return jax.shard_map(
        per_device, mesh=split, in_specs=in_specs, out_specs=out_specs, check_vma=False
    )
```

profile of v0, /device:TPU:1, one launch (start us, length us, event | category | flops | bytes accessed | tf_op | source)
XLA Modules:
  0.0 224.9 jit_solution(15298328586002970351)
XLA Ops:
  7.9 0.7 copy.372
  9.4 0.8 broadcast_reduce_fusion
  10.5 80.9 %all-gather.3.cloned.1.call-done = bf16[32,30,9216]{2,1,0:T(8,128)(2,1)} async-done(((bf16[1,30,9216]{2,1,0:T(8,128)(2,1)}), bf16[32,30,9216]{2,1,0:T(8,128)(2,1)}) %all-gather.3.cloned.1.call-update) | async-done | bytes 17694736 | tf_op jit(solution)/shard_map/all_gather | solution.py:103
  91.4 16.4 %reshape.2849 = bf16[960,9216]{1,0:T(8,128)(2,1)} reshape(bf16[32,30,9216]{2,1,0:T(8,128)(2,1)} %all-gather.3.cloned.1.call-done) | data formatting | bytes 35389440
  107.8 15.0 %convolution_convert_fusion.1 = bf16[384,960]{0,1:T(8,128)(2,1)S(1)} fusion(bf16[384,9216]{1,0:T(8,128)(2,1)} %param.5, bf16[960,9216]{1,0:T(8,128)(2,1)} %reshape.2849), kind=kOutput, calls=%fused_computation.3 | convolution fusion | flops 6795141120 | bytes 25509888 | tf_op jit(solution)/shard_map/dot_general | solution.py:101
  123.6 2.5 %convolution_convert_fusion = bf16[768,1280]{1,0:T(8,128)(2,1)} fusion(bf16[768,480]{1,0:T(8,128)(2,1)S(1)} %reshape.2843, s32[1280]{0:T(1024)S(1)} %add.35, pred[1280]{0:T(1024)(128)(4,1)S(1)} %lt.38), kind=kOutput, calls=%fused_computation | convolution fusion | flops 945930240 | bytes 2709760 | tf_op jit(solution)/shard_map/dot_general | solution.py:108
  126.2 2.7 %copy.373 = bf16[768,1280]{0,1:T(8,128)(2,1)S(1)} copy(bf16[768,1280]{1,0:T(8,128)(2,1)} %convolution_convert_fusion) | data formatting | bytes 3932160 | tf_op jit(solution)/shard_map/convert_element_type | solution.py:108
  129.7 15.1 %all_to_all.20 = f32[8,16,10,80]{3,1,2,0:T(8,128)S(1)} all-to-all(f32[8,16,10,80]{3,1,2,0:T(8,128)S(1)} %bitcast.97), channel_id=1, replica_groups=mesh['img_0'=4,'img_1'=4,'img_2'=2,'grp'=4] {'img_2','grp'}, dimensions={0} | all-to-all | bytes 819200 | tf_op jit(solution)/shard_map/all_to_all | solution.py:25
  145.1 11.1 %all_to_all.21 = f32[16,1,800]{2,1,0:T(1,128)S(1)} all-to-all(f32[16,1,800]{2,1,0:T(1,128)S(1)} %reshape.2863), channel_id=1, replica_groups=mesh['img_0'=4,'img_1'=4,'img_2'=2,'grp'=4] {'img_0','img_1'}, dimensions={0} | all-to-all | bytes 102400 | tf_op jit(solution)/shard_map/all_to_all | solution.py:33
  156.7 0.8 reduce.9
  157.7 0.8 reshape.2865
  158.4 3.5 %all-to-all-start.2 = ((f32[16,1,800]{2,1,0:T(1,128)}), f32[16,1,800]{2,1,0:T(1,128)S(1)}, u32[]{:S(2)}, u32[]{:S(2)}) async-start(f32[16,1,800]{2,1,0:T(1,128)} %reshape.2865), calls=%async_computation.2 | async-start | bytes 114688 | tf_op jit(solution)/shard_map/all_to_all | solution.py:44
  162.0 6.4 %all-to-all-done.2 = f32[16,1,800]{2,1,0:T(1,128)S(1)} async-done(((f32[16,1,800]{2,1,0:T(1,128)}), f32[16,1,800]{2,1,0:T(1,128)S(1)}, u32[]{:S(2)}, u32[]{:S(2)}) %all-to-all-start.2) | async-done | bytes 51232 | tf_op jit(solution)/shard_map/all_to_all | solution.py:44
  168.4 0.8 reduce.10
  169.3 0.9 broadcast_in_dim.121
  170.2 6.4 %all-to-all-start.3 = ((f32[8,16,10,80]{3,1,2,0:T(8,128)}), f32[8,16,10,80]{3,1,2,0:T(8,128)S(1)}, u32[]{:S(2)}, u32[]{:S(2)}) async-start(f32[8,16,10,80]{3,1,2,0:T(8,128)} %broadcast_in_dim.121), calls=%async_computation.3 | async-start | bytes 1310720 | tf_op jit(solution)/shard_map/all_to_all | solution.py:44
  176.7 10.7 %all-to-all-done.3 = f32[8,16,10,80]{3,1,2,0:T(8,128)S(1)} async-done(((f32[8,16,10,80]{3,1,2,0:T(8,128)}), f32[8,16,10,80]{3,1,2,0:T(8,128)S(1)}, u32[]{:S(2)}, u32[]{:S(2)}) %all-to-all-start.3) | async-done | bytes 409632 | tf_op jit(solution)/shard_map/all_to_all | solution.py:44
  187.4 1.3 fusion.6
  193.1 1.3 fusion.8
  198.8 1.3 fusion.10
  204.6 1.3 fusion.4
  205.9 0.7 fusion.12
  206.9 4.9 %copy.407 = f32[768,16,8]{2,1,0:T(8,128)} copy(f32[768,16,8]{0,2,1:T(8,128)S(1)} %convolution_bitcast_fusion) | data formatting | bytes 786432 | tf_op jit(solution)/shard_map/rli,lij->rlj/transpose | solution.py:117
  211.8 6.3 %reshape.2847 = f32[384,256]{1,0:T(8,128)} reshape(f32[768,16,8]{2,1,0:T(8,128)} %copy.407) | data formatting | bytes 786432 | tf_op jit(solution)/shard_map/reshape | solution.py:118
  (130 shorter events, 17.9 us)
Async XLA Ops:
  7.2 84.2 %all-gather.3.cloned.1.call-start = ((), (), s32[]{:S(2)}) async-start(), calls=%async_computation.4 | async-start | bytes 19464192 | tf_op jit(solution)/shard_map/all_gather | solution.py:103
  129.5 32.4 %copy-start.1 = (s32[16]{0:T(128)S(1)}, s32[16]{0:T(128)}, u32[]{:S(2)}) copy-start(s32[16]{0:T(128)} %param.7) | copy-start | bytes 196
  144.8 31.8 %copy-start.2 = (s32[16]{0:T(128)S(1)}, s32[16]{0:T(128)}, u32[]{:S(2)}) copy-start(s32[16]{0:T(128)} %param.8) | copy-start | bytes 196
  144.8 42.6 %copy-start = (f32[16,80,8]{1,2,0:T(8,128)S(1)}, f32[16,80,8]{1,2,0:T(8,128)}, u32[]{:S(2)}) copy-start(f32[16,80,8]{1,2,0:T(8,128)} %param.9) | copy-start | bytes 122884
  158.4 10.0 %all-to-all-start.2 = ((f32[16,1,800]{2,1,0:T(1,128)}), f32[16,1,800]{2,1,0:T(1,128)S(1)}, u32[]{:S(2)}, u32[]{:S(2)}) async-start(f32[16,1,800]{2,1,0:T(1,128)} %reshape.2865), calls=%async_computation.2 | async-start | bytes 114688 | tf_op jit(solution)/shard_map/all_to_all | solution.py:44
  170.2 17.2 %all-to-all-start.3 = ((f32[8,16,10,80]{3,1,2,0:T(8,128)}), f32[8,16,10,80]{3,1,2,0:T(8,128)S(1)}, u32[]{:S(2)}, u32[]{:S(2)}) async-start(f32[8,16,10,80]{3,1,2,0:T(8,128)} %broadcast_in_dim.121), calls=%async_computation.3 | async-start | bytes 1310720 | tf_op jit(solution)/shard_map/all_to_all | solution.py:44
Sparse Core Ops, SparseCore 0:
  10.2 81.1 all-gather.2
where the time goes:
time: 226 us; the launch traced here: 225 us
  waiting for transfers between devices  98.7 us (44%)
  local copies, waits for them, and re-layouts  35.9 us (16%)
  blocking collectives  26.2 us (12%)
  matrix products  23.7 us (10%)
  other arithmetic  15.9 us (7%)
  between operations  14.5 us (6%)
  starting transfers between devices  9.98 us (4%)
    all_gather x1, waiting for transfers between devices, per_device(): lax.all_gather(expansion_basis, IMG, axis=1, tiled=True)  80.9 us
    unnamed x11, local copies, waits for them, and re-layouts  17.5 us
    all_to_all x2, waiting for transfers between devices, sent_to_all(): lax.all_to_all(jnp.broadcast_to(shard[None], (peers, *shard.shape)), axis...  17.1 us
    all_to_all x1, blocking collectives, sum_at_owner(): tiles = lax.all_to_all(cut_along(shard, dim, peers), axis, 0, 0, tiled=True)  15.1 us
    dot_general x1, matrix products, per_device(): jnp.dot(images, lax.all_gather(expansion_basis, IMG, axis=1, tiled=True),...  15 us
    all_to_all x1, blocking collectives, summed_rows(): lax.all_to_all(nearer, far, split_axis=0, concat_axis=0, tiled=True)  11.1 us
    all_to_all x2, starting transfers between devices, sent_to_all(): lax.all_to_all(jnp.broadcast_to(shard[None], (peers, *shard.shape)), axis...  9.94 us
    reduce_sum x30, other arithmetic, subspace(): vector = vector - jnp.sum(earlier * vector, axis=1, keepdims=True) * earlier  6.8 us
  transfers between devices with their start and end apart: 3, of which 3 were waited for; matrix products, arithmetic and copies ran while one was open for 1% of the time, Pallas kernels for 0%

commit v1 on v0

--- a/solution.py
+++ b/solution.py
@@ -1,8 +1,10 @@
+import functools
 import jax
 import jax.numpy as jnp
 from jax import lax
 from jax.sharding import Mesh
 from jax.sharding import PartitionSpec as P
+from jax.lax import all_to_all, axis_size
 
 NMAX = 80
 L = 16
@@ -12,6 +14,16 @@
 IMG = ("img_0", "img_1", "img_2")
 IMG_GRP = ("img_0", "img_1", "img_2", "grp")
 HIGH = lax.Precision.HIGHEST
+
+
+def move_the_shapes(own_rows, d0):
+    mid_arr = axis_size(IMG)
+    outcome_arr = jnp.stack(mid_arr * [own_rows])
+    prior = all_to_all(outcome_arr, IMG, 0, 0)
+    return jnp.concatenate(prior, d0)
+
+
+settle_the_screen = functools.partial(move_the_shapes, d0=1)
 
 
 def cut_along(shard, dim, peers):
@@ -99,9 +111,7 @@
 def per_device(images, expansion_basis, block_sizes, keep_count, start_block):
     rows = images.shape[0]
     coeffs = jnp.dot(
-        images,
-        lax.all_gather(expansion_basis, IMG, axis=1, tiled=True),
-        preferred_element_type=jnp.float32,
+        images, settle_the_screen(expansion_basis), preferred_element_type=jnp.float32
     ).astype(jnp.bfloat16)
     samples = coeffs.reshape(2 * rows, S)
     pick = selector(block_sizes, S, L, NMAX)

time: 226 us -> 449 us (1.99)
  waiting for transfers between devices: 98.7 us -> 279 us
  blocking collectives: 26.2 us -> 67.4 us
  between operations: 14.5 us -> 1.1 us
  starting transfers between devices: 9.98 us -> 19.7 us
  local copies, waits for them, and re-layouts: 35.9 us -> 42.3 us
    all_to_all x0 -> x1, waiting for transfers between devices: none -> 262 us  [move_the_shapes(): prior = all_to_all(outcome_arr, IMG, 0, 0)]
    all_gather x1 -> x0, waiting for transfers between devices: 80.9 us -> none  [per_device(): lax.all_gather(expansion_basis, IMG, axis=1, tiled=True)]
    all_to_all x1, blocking collectives: 11.1 us -> 44.7 us  [summed_rows(): lax.all_to_all(nearer, far, split_axis=0, concat_axis=0, tiled=True)]
    unnamed x11 -> x10, local copies, waits for them, and re-layouts: 17.5 us -> 1.11 us
    reshape x0 -> x1, local copies, waits for them, and re-layouts: none -> 16.4 us  [move_the_shapes(): return jnp.concatenate(prior, d0)]
    all_to_all x0 -> x1, starting transfers between devices: none -> 9.77 us  [move_the_shapes(): prior = all_to_all(outcome_arr, IMG, 0, 0)]
    all_to_all x1, blocking collectives: 15.1 us -> 22.7 us  [sum_at_owner(): tiles = lax.all_to_all(cut_along(shard, dim, peers), axis, 0, 0, tiled=True)]
    another operation x1 -> x2, local copies, waits for them, and re-layouts: 0.73 us -> 7.78 us  [the longest x1 7.69 us: move_the_shapes(): outcome_arr = jnp.stack(mid_arr * [own_rows])]
  transfers between devices with their start and end apart: 3 -> 3, of which waited for: 3 -> 3; matrix products, arithmetic and copies ran while one was open for 1% -> 0% of each run, Pallas kernels for 0% -> 0%
where the time goes in v1:
time: 449 us
  waiting for transfers between devices  279 us (62%)
  blocking collectives  67.4 us (15%)
  local copies, waits for them, and re-layouts  42.3 us (9%)
  matrix products  23.7 us (5%)
  starting transfers between devices  19.7 us (4%)
  other arithmetic  15.3 us (3%)
    all_to_all x1, waiting for transfers between devices, move_the_shapes(): prior = all_to_all(outcome_arr, IMG, 0, 0)  262 us
    all_to_all x1, blocking collectives, summed_rows(): lax.all_to_all(nearer, far, split_axis=0, concat_axis=0, tiled=True)  44.7 us
    all_to_all x1, blocking collectives, sum_at_owner(): tiles = lax.all_to_all(cut_along(shard, dim, peers), axis, 0, 0, tiled=True)  22.7 us
    all_to_all x2, waiting for transfers between devices, sent_to_all(): lax.all_to_all(jnp.broadcast_to(shard[None], (peers, *shard.shape)), axis...  17.1 us
    reshape x1, local copies, waits for them, and re-layouts, move_the_shapes(): return jnp.concatenate(prior, d0)  16.4 us
    dot_general x1, matrix products, per_device(): jnp.dot(images, settle_the_screen(expansion_basis), preferred_element_typ...  15 us
    all_to_all x2, starting transfers between devices, sent_to_all(): lax.all_to_all(jnp.broadcast_to(shard[None], (peers, *shard.shape)), axis...  9.94 us
    all_to_all x1, starting transfers between devices, move_the_shapes(): prior = all_to_all(outcome_arr, IMG, 0, 0)  9.77 us
  transfers between devices with their start and end apart: 3, of which 3 were waited for; matrix products, arithmetic and copies ran while one was open for 0% of the time, Pallas kernels for 0%

profile of v1, /device:TPU:1, one launch (start us, length us, event | category | flops | bytes accessed | tf_op | source)
XLA Modules:
  0.0 448.6 jit_solution(16894954700983877504)
XLA Ops:
  0.6 7.7 %stack.8 = bf16[32,9216,30]{1,2,0:T(8,128)(2,1)} broadcast(bf16[9216,30]{0,1:T(8,128)(2,1)} %param.6), dimensions={1,2} | broadcast | bytes 18247680 | tf_op jit(solution)/shard_map/stack | solution.py:21
  8.3 9.8 %all-to-all-start = ((bf16[32,9216,30]{1,2,0:T(8,128)(2,1)}), bf16[32,9216,30]{1,2,0:T(8,128)(2,1)}, u32[]{:S(2)}, u32[]{:S(2)}) async-start(bf16[32,9216,30]{1,2,0:T(8,128)(2,1)} %stack.8), calls=%async_computation | async-start | bytes 37748736 | tf_op jit(solution)/shard_map/all_to_all | solution.py:22
  18.7 262.0 %all-to-all-done = bf16[32,9216,30]{1,2,0:T(8,128)(2,1)} async-done(((bf16[32,9216,30]{1,2,0:T(8,128)(2,1)}), bf16[32,9216,30]{1,2,0:T(8,128)(2,1)}, u32[]{:S(2)}, u32[]{:S(2)}) %all-to-all-start) | async-done | bytes 17694752 | tf_op jit(solution)/shard_map/all_to_all | solution.py:22
  280.7 16.4 %reshape.2852 = bf16[9216,960]{0,1:T(8,128)(2,1)} reshape(bf16[9216,32,30]{0,2,1:T(8,128)(2,1)} %bitcast) | data formatting | bytes 35389440 | tf_op jit(solution)/shard_map/reshape | solution.py:23
  297.1 15.0 %convolution_convert_fusion.1 = bf16[384,960]{0,1:T(8,128)(2,1)S(1)} fusion(bf16[384,9216]{1,0:T(8,128)(2,1)} %param.5, bf16[9216,960]{0,1:T(8,128)(2,1)} %reshape.2852), kind=kOutput, calls=%fused_computation.3 | convolution fusion | flops 6795141120 | bytes 25509888 | tf_op jit(solution)/shard_map/dot_general | solution.py:113
  312.9 2.5 convolution_convert_fusion
  315.5 2.7 copy.374
  319.1 22.7 %all_to_all.25 = f32[8,16,10,80]{3,1,2,0:T(8,128)S(1)} all-to-all(f32[8,16,10,80]{3,1,2,0:T(8,128)S(1)} %bitcast.97), channel_id=1, replica_groups=mesh['img_0'=4,'img_1'=4,'img_2'=2,'grp'=4] {'img_2','grp'}, dimensions={0} | all-to-all | bytes 819200 | tf_op jit(solution)/shard_map/all_to_all | solution.py:37
  342.0 44.7 %all_to_all.26 = f32[16,1,800]{2,1,0:T(1,128)S(1)} all-to-all(f32[16,1,800]{2,1,0:T(1,128)S(1)} %reshape.2871), channel_id=1, replica_groups=mesh['img_0'=4,'img_1'=4,'img_2'=2,'grp'=4] {'img_0','img_1'}, dimensions={0} | all-to-all | bytes 102400 | tf_op jit(solution)/shard_map/all_to_all | solution.py:45
  387.2 0.8 reduce.9
  388.2 0.8 reshape.2873
  388.9 3.5 all-to-all-start.3
  392.5 6.4 %all-to-all-done.3 = f32[16,1,800]{2,1,0:T(1,128)S(1)} async-done(((f32[16,1,800]{2,1,0:T(1,128)}), f32[16,1,800]{2,1,0:T(1,128)S(1)}, u32[]{:S(2)}, u32[]{:S(2)}) %all-to-all-start.3) | async-done | bytes 51232 | tf_op jit(solution)/shard_map/all_to_all | solution.py:56
  398.9 0.8 reduce.10
  399.8 0.9 broadcast_in_dim.121
  400.7 6.4 %all-to-all-start.4 = ((f32[8,16,10,80]{3,1,2,0:T(8,128)}), f32[8,16,10,80]{3,1,2,0:T(8,128)S(1)}, u32[]{:S(2)}, u32[]{:S(2)}) async-start(f32[8,16,10,80]{3,1,2,0:T(8,128)} %broadcast_in_dim.121), calls=%async_computation.4 | async-start | bytes 1310720 | tf_op jit(solution)/shard_map/all_to_all | solution.py:56
  407.2 10.7 %all-to-all-done.4 = f32[8,16,10,80]{3,1,2,0:T(8,128)S(1)} async-done(((f32[8,16,10,80]{3,1,2,0:T(8,128)}), f32[8,16,10,80]{3,1,2,0:T(8,128)S(1)}, u32[]{:S(2)}, u32[]{:S(2)}) %all-to-all-start.4) | async-done | bytes 409632 | tf_op jit(solution)/shard_map/all_to_all | solution.py:56
  417.9 1.3 fusion.6
  423.6 1.3 fusion.8
  429.3 1.3 fusion.10
  435.1 1.3 fusion.4
  436.4 0.7 fusion.12
  437.4 4.9 %copy.408 = f32[768,16,8]{2,1,0:T(8,128)} copy(f32[768,16,8]{0,2,1:T(8,128)S(1)} %convolution_bitcast_fusion) | data formatting | bytes 786432 | tf_op jit(solution)/shard_map/rli,lij->rlj/transpose | solution.py:127
  442.3 6.3 %reshape.2857 = f32[384,256]{1,0:T(8,128)} reshape(f32[768,16,8]{2,1,0:T(8,128)} %copy.408) | data formatting | bytes 786432 | tf_op jit(solution)/shard_map/reshape | solution.py:128
  (130 shorter events, 16.7 us)
Async XLA Ops:
  8.3 9.8 %copy-start.1 = (s32[16]{0:T(128)S(1)}, s32[16]{0:T(128)}, u32[]{:S(2)}) copy-start(s32[16]{0:T(128)} %param.7) | copy-start | bytes 196
  8.3 272.4 %all-to-all-start = ((bf16[32,9216,30]{1,2,0:T(8,128)(2,1)}), bf16[32,9216,30]{1,2,0:T(8,128)(2,1)}, u32[]{:S(2)}, u32[]{:S(2)}) async-start(bf16[32,9216,30]{1,2,0:T(8,128)(2,1)} %stack.8), calls=%async_computation | async-start | bytes 37748736 | tf_op jit(solution)/shard_map/all_to_all | solution.py:22
  341.8 65.3 %copy-start.2 = (s32[16]{0:T(128)S(1)}, s32[16]{0:T(128)}, u32[]{:S(2)}) copy-start(s32[16]{0:T(128)} %param.8) | copy-start | bytes 196
  341.8 76.1 %copy-start = (f32[16,80,8]{1,2,0:T(8,128)S(1)}, f32[16,80,8]{1,2,0:T(8,128)}, u32[]{:S(2)}) copy-start(f32[16,80,8]{1,2,0:T(8,128)} %param.9) | copy-start | bytes 122884
  388.9 10.0 %all-to-all-start.3 = ((f32[16,1,800]{2,1,0:T(1,128)}), f32[16,1,800]{2,1,0:T(1,128)S(1)}, u32[]{:S(2)}, u32[]{:S(2)}) async-start(f32[16,1,800]{2,1,0:T(1,128)} %reshape.2873), calls=%async_computation.3 | async-start | bytes 114688 | tf_op jit(solution)/shard_map/all_to_all | solution.py:56
  400.7 17.2 %all-to-all-start.4 = ((f32[8,16,10,80]{3,1,2,0:T(8,128)}), f32[8,16,10,80]{3,1,2,0:T(8,128)S(1)}, u32[]{:S(2)}, u32[]{:S(2)}) async-start(f32[8,16,10,80]{3,1,2,0:T(8,128)} %broadcast_in_dim.121), calls=%async_computation.4 | async-start | bytes 1310720 | tf_op jit(solution)/shard_map/all_to_all | solution.py:56
